TPU v7x, 32 devices: a whole 2x2x4 slice. The times are simulated.
32 devices in a mesh: pts: 8 (over y, x, core), wlk: 4 (over z).
Axes of the slice: x: 2, y: 2, z: 4, core: 2. Of those that a mesh axis runs over, the one named last changes fastest.
Arguments:
- green_half: bfloat16 [8, 400, 2400], P('wlk'), may hold values from -6 to 6
- collocation: bfloat16 [2400, 9600], P('wlk', 'pts'), may hold values from -0.125 to 0.125
- occupied: bfloat16 [9600, 400], P('pts'), may hold values from -0.0029296875 to 0.0029296875
- kernel: bfloat16 [9600, 9600], P('pts'), may hold values from 0 to 16, as said below
Outputs:
- potential: float32 [8, 9600], P('wlk', 'pts')
- coulomb_energy: float32 [8], P('wlk')
- exchange_energy: float32 [8], P('wlk')
Inputs may be any that keep to these rules, and one draw needn't show every extreme that they name: kernel is symmetric and positive definite: kernel[p, q] equals kernel[q, p].
All inputs are finite; a program needn't handle non-finite values.
Results may differ from a plain program's by a relative error of at most 0.008.
Values may be sent and summed in bfloat16 or wider, within the bound.
A program may use at most 192 MiB of HBM per device.

v0:
```python
import jax
import jax.numpy as jnp
from jax import lax
from jax.sharding import PartitionSpec as P


def passed_along(block, axis, distance):
    devices = range(lax.axis_size(axis))
    route = [((i - distance) % len(devices), i) for i in devices]
    return lax.ppermute(block, axis, route)


def local(green_half, collocation, occupied, kernel):
    pts_rows = occupied.shape[0]
    theta = jnp.einsum(
        "mp,wim->pwi",
        lax.all_gather(collocation, "wlk", axis=0, tiled=True),
        green_half,
        preferred_element_type=jnp.float32,
    ).astype(jnp.bfloat16)
    density = jnp.einsum("pwi,pi->wp", theta, occupied, preferred_element_type=jnp.float32)
    density_b = density.astype(jnp.bfloat16)

    def block_terms(start, theta_far, occ_far):
        cross_near = jnp.einsum("awi,bi->wab", theta, occ_far, preferred_element_type=jnp.float32)
        cross_far = jnp.einsum(
            "ai,bwi->wab", occupied, theta_far, preferred_element_type=jnp.float32
        )
        kernel_part = lax.dynamic_slice_in_dim(kernel, start, occ_far.shape[0], 1).astype(
            jnp.float32
        )
        return jnp.sum(kernel_part[None] * cross_near * cross_far, axis=(1, 2))

    density_all = lax.all_gather(density_b, "pts", axis=1, tiled=True)
    potential = jnp.einsum("wq,aq->wa", density_all, kernel, preferred_element_type=jnp.float32)
    devices = lax.axis_size("pts")
    position = lax.axis_index("pts")
    exchange_sum = block_terms(position * pts_rows, theta, occupied)
    travel = (theta, occupied)
    for stride in range(1, devices // 2 + 1):
        travel = passed_along((travel[0], travel[1]), "pts", 1)
        source = (position - stride) % devices
        weight = 1.0 if 2 * stride == devices else 2.0
        exchange_sum = exchange_sum + weight * block_terms(source * pts_rows, travel[0], travel[1])
    coulomb = 0.5 * jnp.sum(density * potential, axis=1)
    coulomb_energy, exchange_energy = lax.psum((coulomb, -0.5 * exchange_sum), "pts")
    return (potential, coulomb_energy, exchange_energy)


def solution(mesh):
    placed = (P("wlk", None, None), P("wlk", "pts"), P("pts", None), P("pts", None))
    return jax.shard_map(
        local,
        mesh=mesh,
        in_specs=placed,
        out_specs=(P("wlk", "pts"), P("wlk"), P("wlk")),
        check_vma=False,
    )
```

profile of v0, /device:TPU:0, one launch (start us, length us, event | category | flops | bytes accessed | tf_op | source)
XLA Modules:
  0.0 310.9 jit_solution(14020435606796289344)
XLA Ops:
  7.2 0.0 all-gather.3.cloned.1.call-start
  7.2 0.7 all-gather.3.cloned.1.call-update
  7.9 0.5 collective-permute-start
  8.4 15.3 %collective-permute-done = bf16[1200,400]{0,1:T(8,128)(2,1)S(1)} collective-permute-done((bf16[1200,400]{0,1:T(8,128)(2,1)}, bf16[1200,400]{0,1:T(8,128)(2,1)S(1)}, u32[]{:S(2)}, u32[]{:S(2)}) %collective-permute-start) | collective-permute-done | bytes 960032 | tf_op jit(solution)/shard_map/ppermute | solution.py:10
  23.7 0.0 copy-start.3
  23.7 0.0 collective-permute-start.2
  23.8 3.1 convert.2
  26.8 11.8 %collective-permute-done.2 = bf16[1200,400]{0,1:T(8,128)(2,1)S(1)} collective-permute-done((bf16[1200,400]{0,1:T(8,128)(2,1)S(1)}, bf16[1200,400]{0,1:T(8,128)(2,1)S(1)}, u32[]{:S(2)}, u32[]{:S(2)}) %collective-permute-start.2) | collective-permute-done | bytes 960032 | tf_op jit(solution)/shard_map/ppermute | solution.py:10
  38.6 0.0 copy-start.1
  38.6 0.0 collective-permute-start.4
  38.6 0.0 copy-done.3
  38.6 86.6 %all-gather.3.cloned.1.call-done = bf16[2400,1200]{1,0:T(8,128)(2,1)} async-done(((bf16[600,1200]{1,0:T(8,128)(2,1)}), bf16[2400,1200]{1,0:T(8,128)(2,1)}) %all-gather.3.cloned.1.call-update) | async-done | bytes 5760016 | tf_op jit(solution)/shard_map/all_gather | solution.py:17
  125.2 9.4 %multiply_reduce_fusion = (f32[1200,2]{0,1:T(2,128)S(1)}, bf16[1200,2,400]{0,2,1:T(8,128)(2,1)S(1)}) fusion(f32[1200,400]{0,1:T(8,128)} %convert.2, bf16[2,400,2400]{2,1,0:T(8,128)(2,1)} %param.4, bf16[2400,1200]{1,0:T(8,128)(2,1)} %all-gather.3.cloned.1.call-done), kind=kOutput, calls=%fused_computation.20 | convolution fusion | flops 4611837440 | bytes 13449600 | tf_op jit(solution)/shard_map/mp,wim->pwi/dot_general | solution.py:15
  134.6 0.0 copy-done.1
  134.6 0.1 collective-permute-start.1
  134.7 17.5 %dynamic-slice_convert_fusion.3 = (f32[1200,1200]{1,0:T(8,128)}, f32[1200,1200]{1,0:T(8,128)}, f32[1200,1200]{1,0:T(8,128)}, f32[1200,1200]{1,0:T(8,128)}, f32[1200,1200]{1,0:T(8,128)}) fusion(bf16[1200,9600]{1,0:T(8,128)(2,1)} %param.7, s32[]{:T(128)S(6)} %select_n.36, s32[]{:T(128)S(6)} %select_n.38, s32[]{:T(128)S(6)} %select_n.34, s32[]{:T(128)S(6)} %select_n.42, ...), kind=kLoop, calls=%fused_computation.25 | loop fusion | flops 7200000 | bytes 43200020 | tf_op jit(solution)/shard_map/convert_element_type | solution.py:29
  152.1 7.8 %copy.21 = f32[1200,1200]{0,1:T(8,128)} copy(f32[1200,1200]{1,0:T(8,128)} %get-tuple-element.7) | data formatting | bytes 11520000 | tf_op jit(solution)/shard_map/convert_element_type | solution.py:29
  160.0 0.0 collective-permute-done.4
  160.0 1.5 collective-permute-start.6
  161.5 16.0 %all-gather = bf16[8,1200,2]{1,2,0:T(2,128)(2,1)S(1)} all-gather(bf16[1,1200,2]{1,2,0:T(2,128)(2,1)S(1)} %fusion.29), channel_id=1, replica_groups=mesh['pts'=8,'wlk'=4] {'pts'}, dimensions={0}, use_global_device_ids=true | all-gather | bytes 43200 | tf_op jit(solution)/shard_map/all_gather | solution.py:34
  177.6 0.2 reshape.12
  177.7 0.0 copy-start
  177.7 11.5 %fusion.28 = (f32[2]{0:T(128)S(1)}, f32[2,1200]{1,0:T(2,128)}) fusion(f32[1200,2]{0,1:T(2,128)S(1)} %get-tuple-element.10, bf16[9600,2]{0,1:T(2,128)(2,1)S(1)} %reshape.12, bf16[1200,9600]{1,0:T(8,128)(2,1)} %param.7), kind=kOutput, calls=%fused_computation.43 | convolution fusion | flops 46084800 | bytes 23097608 | tf_op jit(solution)/shard_map/wq,aq->wa/dot_general | solution.py:35
  189.2 0.0 collective-permute-done.1
  189.2 0.4 collective-permute-start.3
  189.6 0.0 copy-done
  189.6 6.3 %fusion.26 = f32[1200,2,1200]{2,0,1:T(8,128)} fusion(bf16[1200,2,400]{0,2,1:T(8,128)(2,1)S(1)} %get-tuple-element.11, bf16[1200,400]{0,1:T(8,128)(2,1)S(1)} %copy-done), kind=kOutput, calls=%fused_computation.39 | convolution fusion | flops 2304000000 | bytes 14400000 | tf_op jit(solution)/shard_map/awi,bi->wab/dot_general | solution.py:25
  195.9 13.4 %copy.22 = f32[1200,2,1200]{0,2,1:T(8,128)} copy(f32[1200,2,1200]{2,0,1:T(8,128)} %fusion.26) | data formatting | bytes 23040000 | tf_op jit(solution)/shard_map/awi,bi->wab/dot_general | solution.py:25
  209.3 0.0 slice-start.6
  209.3 10.9 %fusion.8 = f32[2]{0:T(128)S(1)} fusion(f32[1200,2,1200]{2,0,1:T(8,128)} %fusion.26, f32[1200,2,1200]{0,2,1:T(8,128)} %copy.22, f32[1200,1200]{0,1:T(8,128)} %copy.21), kind=kLoop, calls=%fused_computation.17 | loop fusion | flops 8639998 | bytes 28800008 | tf_op jit(solution)/shard_map/reduce_sum | solution.py:32
  220.3 0.0 slice-start.7
  220.3 0.0 copy-start.4
  220.3 0.0 collective-permute-done.3
  220.3 1.5 collective-permute-start.5
  221.8 8.0 %convolution_bitcast_fusion.3 = f32[2,1200,1200]{2,1,0:T(8,128)} fusion(bf16[1200,2,400]{0,2,1:T(8,128)(2,1)} %collective-permute-done.1, bf16[1200,400]{0,1:T(8,128)(2,1)S(1)} %copy-done), kind=kOutput, calls=%fused_computation.15 | convolution fusion | flops 2304000000 | bytes 14400000 | tf_op jit(solution)/shard_map/ai,bwi->wab/dot_general | solution.py:26
  229.8 0.0 slice-done.6
  229.8 0.0 slice-done.7
  229.8 0.0 copy-done.4
  229.8 0.0 slice-start.4
  229.8 8.6 %fusion.17 = f32[2]{0:T(128)S(1)} fusion(f32[2,1200,1200]{2,1,0:T(8,128)} %convolution_bitcast_fusion.3, bf16[1200,2,400]{0,2,1:T(8,128)(2,1)S(1)} %get-tuple-element.11, f32[1200,1200]{1,0:T(8,128)S(1)} %bitcast.102, bf16[1200,400]{0,1:T(8,128)(2,1)S(1)} %copy-done.4), kind=kOutput, calls=%fused_computation.30 | convolution fusion | flops 2312640000 | bytes 20160008 | tf_op jit(solution)/shard_map/awi,bi->wab/dot_general | solution.py:25
  238.4 0.0 slice-start.5
  238.4 0.0 copy-start.2
  238.4 8.2 %convolution_bitcast_fusion.2 = f32[2,1200,1200]{2,1,0:T(8,128)} fusion(bf16[1200,2,400]{0,2,1:T(8,128)(2,1)} %collective-permute-done.3, bf16[1200,400]{0,1:T(8,128)(2,1)S(1)} %copy-done), kind=kOutput, calls=%fused_computation.14 | convolution fusion | flops 2304000000 | bytes 14400000 | tf_op jit(solution)/shard_map/ai,bwi->wab/dot_general | solution.py:26
  246.6 0.0 collective-permute-done.5
  246.6 0.3 collective-permute-start.7
  246.9 0.0 slice-done.4
  246.9 0.0 slice-done.5
  246.9 0.0 copy-done.2
  246.9 0.0 slice-start.2
  246.9 8.6 %fusion.16 = f32[2]{0:T(128)S(1)} fusion(f32[2,1200,1200]{2,1,0:T(8,128)} %convolution_bitcast_fusion.2, bf16[1200,2,400]{0,2,1:T(8,128)(2,1)S(1)} %get-tuple-element.11, f32[1200,1200]{1,0:T(8,128)S(1)} %bitcast.100, bf16[1200,400]{0,1:T(8,128)(2,1)S(1)} %copy-done.2), kind=kOutput, calls=%fused_computation.29 | convolution fusion | flops 2312640000 | bytes 20160008 | tf_op jit(solution)/shard_map/awi,bi->wab/dot_general | solution.py:25
  255.5 0.0 slice-start.3
  255.5 8.1 %convolution_bitcast_fusion.1 = f32[2,1200,1200]{2,1,0:T(8,128)} fusion(bf16[1200,2,400]{0,2,1:T(8,128)(2,1)} %collective-permute-done.5, bf16[1200,400]{0,1:T(8,128)(2,1)S(1)} %copy-done), kind=kOutput, calls=%fused_computation.13 | convolution fusion | flops 2304000000 | bytes 14400000 | tf_op jit(solution)/shard_map/ai,bwi->wab/dot_general | solution.py:26
  263.6 0.0 slice-done.2
  263.6 0.0 slice-done.3
  263.6 0.0 slice-start
  263.6 8.9 %fusion.15 = f32[2]{0:T(128)S(1)} fusion(f32[2,1200,1200]{2,1,0:T(8,128)} %convolution_bitcast_fusion.1, bf16[1200,2,400]{0,2,1:T(8,128)(2,1)S(1)} %get-tuple-element.11, f32[1200,1200]{1,0:T(8,128)S(1)} %bitcast.98, bf16[1200,400]{0,1:T(8,128)(2,1)} %collective-permute-done.4), kind=kOutput, calls=%fused_computation.28 | convolution fusion | flops 2312640000 | bytes 20160008 | tf_op jit(solution)/shard_map/awi,bi->wab/dot_general | solution.py:25
  272.5 0.0 slice-start.1
  272.5 0.2 collective-permute-done.7
  272.7 8.1 %convolution_bitcast_fusion = f32[2,1200,1200]{2,1,0:T(8,128)} fusion(bf16[1200,2,400]{0,2,1:T(8,128)(2,1)} %collective-permute-done.7, bf16[1200,400]{0,1:T(8,128)(2,1)S(1)} %copy-done), kind=kOutput, calls=%fused_computation.12 | convolution fusion | flops 2304000000 | bytes 14400000 | tf_op jit(solution)/shard_map/ai,bwi->wab/dot_general | solution.py:26
  280.8 0.0 collective-permute-done.6
  280.8 0.0 slice-done
  280.8 0.0 slice-done.1
  280.8 8.7 %fusion.14 = f32[2]{0:T(128)S(1)} fusion(f32[2,1200,1200]{2,1,0:T(8,128)} %convolution_bitcast_fusion, bf16[1200,2,400]{0,2,1:T(8,128)(2,1)S(1)} %get-tuple-element.11, f32[1200,1200]{1,0:T(8,128)S(1)} %bitcast.96, bf16[1200,400]{0,1:T(8,128)(2,1)} %collective-permute-done.6), kind=kOutput, calls=%fused_computation.27 | convolution fusion | flops 2312640000 | bytes 20160008 | tf_op jit(solution)/shard_map/awi,bi->wab/dot_general | solution.py:25
  289.6 14.5 %all-reduce = (f32[2]{0:T(128)}, f32[2]{0:T(128)}) all-reduce(f32[2]{0:T(128)S(1)} %broadcast_multiply_fusion, f32[2]{0:T(128)S(1)} %add_multiply_fusion), channel_id=1, replica_groups=mesh['pts'=8,'wlk'=4] {'pts'}, use_global_device_ids=true, to_apply=%region_1.2 | all-reduce | flops 4 | bytes 32 | tf_op jit(solution)/shard_map/psum | solution.py:46
  (8 shorter events, 0.0 us)
Async XLA Ops:
  7.2 118.0 %all-gather.3.cloned.1.call-start = ((), (), s32[]{:S(2)}) async-start(), calls=%async_computation | async-start | bytes 7680000 | tf_op jit(solution)/shard_map/all_gather | solution.py:17
  7.9 15.8 %collective-permute-start = (bf16[1200,400]{0,1:T(8,128)(2,1)}, bf16[1200,400]{0,1:T(8,128)(2,1)S(1)}, u32[]{:S(2)}, u32[]{:S(2)}) collective-permute-start(bf16[1200,400]{0,1:T(8,128)(2,1)} %param.6), channel_id=1, source_target_pairs={{28,0},{0,4},{4,8},{8,12},{12,16},{16,20},{20,24},{24,28},{29,1},{... | collective-permute-start | bytes 2880008 | tf_op jit(solution)/shard_map/ppermute | solution.py:10
  23.7 14.9 %copy-start.3 = (bf16[1200,400]{0,1:T(8,128)(2,1)}, bf16[1200,400]{0,1:T(8,128)(2,1)S(1)}, u32[]{:S(2)}) copy-start(bf16[1200,400]{0,1:T(8,128)(2,1)S(1)} %collective-permute-done) | copy-start | bytes 2880004
  23.7 14.9 %collective-permute-start.2 = (bf16[1200,400]{0,1:T(8,128)(2,1)S(1)}, bf16[1200,400]{0,1:T(8,128)(2,1)S(1)}, u32[]{:S(2)}, u32[]{:S(2)}) collective-permute-start(bf16[1200,400]{0,1:T(8,128)(2,1)S(1)} %collective-permute-done), channel_id=1, source_target_pairs={{28,0},{0,4},{4,8},{8,12},{12,16},{16,20},{20,24},{24,28},{29,1},{... | collective-permute-start | bytes 2880008 | tf_op jit(solution)/shard_map/ppermute | solution.py:10
  38.6 96.0 %copy-start.1 = (bf16[1200,400]{0,1:T(8,128)(2,1)}, bf16[1200,400]{0,1:T(8,128)(2,1)S(1)}, u32[]{:S(2)}) copy-start(bf16[1200,400]{0,1:T(8,128)(2,1)S(1)} %collective-permute-done.2) | copy-start | bytes 2880004
  38.6 121.4 %collective-permute-start.4 = (bf16[1200,400]{0,1:T(8,128)(2,1)S(1)}, bf16[1200,400]{0,1:T(8,128)(2,1)}, u32[]{:S(2)}, u32[]{:S(2)}) collective-permute-start(bf16[1200,400]{0,1:T(8,128)(2,1)S(1)} %collective-permute-done.2), channel_id=1, source_target_pairs={{28,0},{0,4},{4,8},{8,12},{12,16},{16,20},{20,24},{24,28},{29,1},{... | collective-permute-start | bytes 2880008 | tf_op jit(solution)/shard_map/ppermute | solution.py:10
  134.6 54.6 %collective-permute-start.1 = (bf16[1200,2,400]{0,2,1:T(8,128)(2,1)S(1)}, bf16[1200,2,400]{0,2,1:T(8,128)(2,1)}, u32[]{:S(2)}, u32[]{:S(2)}) collective-permute-start(bf16[1200,2,400]{0,2,1:T(8,128)(2,1)S(1)} %get-tuple-element.11), channel_id=1, source_target_pairs={{28,0},{0,4},{4,8},{8,12},{12,16},{16,20},{20,24},{24,28},{29,1},{... | collective-permute-start | bytes 5760008 | tf_op jit(solution)/shard_map/ppermute | solution.py:10
  160.0 120.9 %collective-permute-start.6 = (bf16[1200,400]{0,1:T(8,128)(2,1)}, bf16[1200,400]{0,1:T(8,128)(2,1)}, u32[]{:S(2)}, u32[]{:S(2)}) collective-permute-start(bf16[1200,400]{0,1:T(8,128)(2,1)} %collective-permute-done.4), channel_id=1, source_target_pairs={{28,0},{0,4},{4,8},{8,12},{12,16},{16,20},{20,24},{24,28},{29,1},{... | collective-permute-start | bytes 2880008 | tf_op jit(solution)/shard_map/ppermute | solution.py:10
  177.7 11.9 %copy-start = (bf16[1200,400]{0,1:T(8,128)(2,1)S(1)}, bf16[1200,400]{0,1:T(8,128)(2,1)}, u32[]{:S(2)}) copy-start(bf16[1200,400]{0,1:T(8,128)(2,1)} %param.6) | copy-start | bytes 2880004
  189.2 31.0 %collective-permute-start.3 = (bf16[1200,2,400]{0,2,1:T(8,128)(2,1)}, bf16[1200,2,400]{0,2,1:T(8,128)(2,1)}, u32[]{:S(2)}, u32[]{:S(2)}) collective-permute-start(bf16[1200,2,400]{0,2,1:T(8,128)(2,1)} %collective-permute-done.1), channel_id=1, source_target_pairs={{28,0},{0,4},{4,8},{8,12},{12,16},{16,20},{20,24},{24,28},{29,1},{... | collective-permute-start | bytes 5760008 | tf_op jit(solution)/shard_map/ppermute | solution.py:10
  209.3 20.4 %slice-start.6 = ((s8[6144000]{0:T(1024)(128)(4,1)}), s8[4194304]{0:T(1024)(128)(4,1)S(1)}, s32[]{:S(2)}) async-start(s8[6144000]{0:T(1024)(128)(4,1)} %bitcast.101), calls=%async_computation.7 | async-start | bytes 8388608
  220.3 9.5 %slice-start.7 = ((s8[6144000]{0:T(1024)(128)(4,1)}), s8[1949696]{0:T(1024)(128)(4,1)S(1)}, s32[]{:S(2)}) async-start(s8[6144000]{0:T(1024)(128)(4,1)} %bitcast.101), calls=%async_computation.8 | async-start | bytes 3899392
  220.3 9.5 %copy-start.4 = (bf16[1200,400]{0,1:T(8,128)(2,1)S(1)}, bf16[1200,400]{0,1:T(8,128)(2,1)}, u32[]{:S(2)}) copy-start(bf16[1200,400]{0,1:T(8,128)(2,1)} %copy-done.3) | copy-start | bytes 2880004
  220.3 26.3 %collective-permute-start.5 = (bf16[1200,2,400]{0,2,1:T(8,128)(2,1)}, bf16[1200,2,400]{0,2,1:T(8,128)(2,1)}, u32[]{:S(2)}, u32[]{:S(2)}) collective-permute-start(bf16[1200,2,400]{0,2,1:T(8,128)(2,1)} %collective-permute-done.3), channel_id=1, source_target_pairs={{28,0},{0,4},{4,8},{8,12},{12,16},{16,20},{20,24},{24,28},{29,1},{... | collective-permute-start | bytes 5760008 | tf_op jit(solution)/shard_map/ppermute | solution.py:10
  229.8 17.1 %slice-start.4 = ((s8[6144000]{0:T(1024)(128)(4,1)}), s8[4194304]{0:T(1024)(128)(4,1)S(1)}, s32[]{:S(2)}) async-start(s8[6144000]{0:T(1024)(128)(4,1)} %bitcast.99), calls=%async_computation.5 | async-start | bytes 8388608
  238.4 8.5 %slice-start.5 = ((s8[6144000]{0:T(1024)(128)(4,1)}), s8[1949696]{0:T(1024)(128)(4,1)S(1)}, s32[]{:S(2)}) async-start(s8[6144000]{0:T(1024)(128)(4,1)} %bitcast.99), calls=%async_computation.6 | async-start | bytes 3899392
  238.4 8.5 %copy-start.2 = (bf16[1200,400]{0,1:T(8,128)(2,1)S(1)}, bf16[1200,400]{0,1:T(8,128)(2,1)}, u32[]{:S(2)}) copy-start(bf16[1200,400]{0,1:T(8,128)(2,1)} %copy-done.1) | copy-start | bytes 2880004
  246.6 26.1 %collective-permute-start.7 = (bf16[1200,2,400]{0,2,1:T(8,128)(2,1)}, bf16[1200,2,400]{0,2,1:T(8,128)(2,1)}, u32[]{:S(2)}, u32[]{:S(2)}) collective-permute-start(bf16[1200,2,400]{0,2,1:T(8,128)(2,1)} %collective-permute-done.5), channel_id=1, source_target_pairs={{28,0},{0,4},{4,8},{8,12},{12,16},{16,20},{20,24},{24,28},{29,1},{... | collective-permute-start | bytes 5760008 | tf_op jit(solution)/shard_map/ppermute | solution.py:10
  246.9 16.7 %slice-start.2 = ((s8[6144000]{0:T(1024)(128)(4,1)}), s8[4194304]{0:T(1024)(128)(4,1)S(1)}, s32[]{:S(2)}) async-start(s8[6144000]{0:T(1024)(128)(4,1)} %bitcast.97), calls=%async_computation.3 | async-start | bytes 8388608
  255.5 8.2 %slice-start.3 = ((s8[6144000]{0:T(1024)(128)(4,1)}), s8[1949696]{0:T(1024)(128)(4,1)S(1)}, s32[]{:S(2)}) async-start(s8[6144000]{0:T(1024)(128)(4,1)} %bitcast.97), calls=%async_computation.4 | async-start | bytes 3899392
  263.6 17.2 %slice-start = ((s8[6144000]{0:T(1024)(128)(4,1)}), s8[4194304]{0:T(1024)(128)(4,1)S(1)}, s32[]{:S(2)}) async-start(s8[6144000]{0:T(1024)(128)(4,1)} %bitcast.95), calls=%async_computation.1 | async-start | bytes 8388608
  272.5 8.3 %slice-start.1 = ((s8[6144000]{0:T(1024)(128)(4,1)}), s8[1949696]{0:T(1024)(128)(4,1)S(1)}, s32[]{:S(2)}) async-start(s8[6144000]{0:T(1024)(128)(4,1)} %bitcast.95), calls=%async_computation.2 | async-start | bytes 3899392
Sparse Core Ops, SparseCore 0:
  9.5 115.6 all-gather.2
where the time goes:
time: 312 us; the launch traced here: 311 us
  waiting for transfers between devices  115 us (37%)
  matrix products  94.4 us (30%)
  other arithmetic  31.5 us (10%)
  blocking collectives  30.5 us (10%)
  local copies, waits for them, and re-layouts  21.5 us (7%)
  between operations  14.1 us (5%)
  starting transfers between devices  4.4 us (1%)
    all_gather x1, waiting for transfers between devices, local(): lax.all_gather(collocation, 'wlk', axis=0, tiled=True)  86.6 us
    dot_general x5, matrix products, block_terms(): jnp.einsum('awi,bi->wab', theta, occ_far, preferred_element_type=jnp.floa...  41.1 us
    dot_general x4, matrix products, block_terms(): jnp.einsum('ai,bwi->wab', occupied, theta_far, preferred_element_type=jnp...  32.4 us
    ppermute x8, waiting for transfers between devices, passed_along(): return lax.ppermute(block, axis, route)  27.3 us
    convert_element_type x1, other arithmetic, block_terms(): lax.dynamic_slice_in_dim(kernel, start, occ_far.shape[0], 1)  17.5 us
    all_gather x1, blocking collectives, local(): density_all = lax.all_gather(density_b, 'pts', axis=1, tiled=True)  16 us
    psum x1, blocking collectives, local(): lax.psum((coulomb, -0.5 * exchange_sum), 'pts')  14.5 us
    dot_general x1, local copies, waits for them, and re-layouts, block_terms(): jnp.einsum('awi,bi->wab', theta, occ_far, preferred_element_type=jnp.floa...  13.4 us
  transfers between devices with their start and end apart: 9, of which 4 were waited for; matrix products, arithmetic and copies ran while one was open for 45% of the time, Pallas kernels for 0%

commit v1 on v0

--- a/solution.py
+++ b/solution.py
@@ -2,6 +2,18 @@
 import jax.numpy as jnp
 from jax import lax
 from jax.sharding import PartitionSpec as P
+
+
+def summed_around(x, axis, dim, contribution):
+    length, index = (lax.axis_size(axis), lax.axis_index(axis))
+    left = [(i, (i - 1) % length) for i in range(length)]
+    span = x.shape[dim]
+    current = x
+    total = contribution(current, index * span)
+    for turn in range(1, length):
+        current = lax.ppermute(current, axis, left)
+        total = total + contribution(current, (index + turn) % length * span)
+    return total
 
 
 def passed_along(block, axis, distance):
@@ -12,11 +24,16 @@
 
 def local(green_half, collocation, occupied, kernel):
     pts_rows = occupied.shape[0]
-    theta = jnp.einsum(
-        "mp,wim->pwi",
-        lax.all_gather(collocation, "wlk", axis=0, tiled=True),
-        green_half,
-        preferred_element_type=jnp.float32,
+    theta = summed_around(
+        collocation,
+        "wlk",
+        0,
+        lambda part, start_2: jnp.einsum(
+            "mp,wim->pwi",
+            part,
+            lax.dynamic_slice_in_dim(green_half, start_2, part.shape[0], axis=2),
+            preferred_element_type=jnp.float32,
+        ),
     ).astype(jnp.bfloat16)
     density = jnp.einsum("pwi,pi->wp", theta, occupied, preferred_element_type=jnp.float32)
     density_b = density.astype(jnp.bfloat16)

time: 312 us -> 286 us (0.917)
  waiting for transfers between devices: 115 us -> 84.5 us
  between operations: 14.1 us -> 0.84 us
  starting transfers between devices: 4.4 us -> 16.7 us
  matrix products: 94.4 us -> 97.9 us
    all_gather x1 -> x0, waiting for transfers between devices: 86.6 us -> none  [local(): lax.all_gather(collocation, 'wlk', axis=0, tiled=True)]
    ppermute x0 -> x3, waiting for transfers between devices: none -> 78.1 us  [summed_around(): current = lax.ppermute(current, axis, left)]
    ppermute x8, waiting for transfers between devices: 27.3 us -> 6.33 us  [passed_along(): return lax.ppermute(block, axis, route)]
    ppermute x0 -> x3, starting transfers between devices: none -> 13.7 us  [summed_around(): current = lax.ppermute(current, axis, left)]
    dot_general x1 -> x4, matrix products: 9.38 us -> 12.8 us  [local(): jnp.einsum('mp,wim->pwi', part, lax.dynamic_slice_in_dim(green_half, star...]
  transfers between devices with their start and end apart: 9 -> 11, of which waited for: 4 -> 5; matrix products, arithmetic and copies ran while one was open for 45% -> 50% of each run, Pallas kernels for 0% -> 0%
where the time goes in v1:
time: 286 us; the launch traced here: 285 us
  matrix products  97.9 us (34%)
  waiting for transfers between devices  84.5 us (30%)
  other arithmetic  32.1 us (11%)
  blocking collectives  31.2 us (11%)
  local copies, waits for them, and re-layouts  21.5 us (8%)
  starting transfers between devices  16.7 us (6%)
    ppermute x3, waiting for transfers between devices, summed_around(): current = lax.ppermute(current, axis, left)  78.1 us
    dot_general x5, matrix products, block_terms(): jnp.einsum('awi,bi->wab', theta, occ_far, preferred_element_type=jnp.floa...  41.1 us
    dot_general x4, matrix products, block_terms(): jnp.einsum('ai,bwi->wab', occupied, theta_far, preferred_element_type=jnp...  32.6 us
    convert_element_type x1, other arithmetic, block_terms(): lax.dynamic_slice_in_dim(kernel, start, occ_far.shape[0], 1)  18.1 us
    all_gather x1, blocking collectives, local(): density_all = lax.all_gather(density_b, 'pts', axis=1, tiled=True)  16.7 us
    psum x1, blocking collectives, local(): lax.psum((coulomb, -0.5 * exchange_sum), 'pts')  14.6 us
    ppermute x3, starting transfers between devices, summed_around(): current = lax.ppermute(current, axis, left)  13.7 us
    dot_general x1, local copies, waits for them, and re-layouts, block_terms(): jnp.einsum('awi,bi->wab', theta, occ_far, preferred_element_type=jnp.floa...  13.4 us
  transfers between devices with their start and end apart: 11, of which 5 were waited for; matrix products, arithmetic and copies ran while one was open for 50% of the time, Pallas kernels for 0%

profile of v1, /device:TPU:0, one launch (start us, length us, event | category | flops | bytes accessed | tf_op | source)
XLA Modules:
  0.0 284.8 jit_solution(14850563744657799469)
XLA Ops:
  0.6 5.1 %collective-permute-start = (bf16[600,1200]{1,0:T(8,128)(2,1)}, bf16[600,1200]{1,0:T(8,128)(2,1)S(1)}, u32[]{:S(2)}, u32[]{:S(2)}) collective-permute-start(bf16[600,1200]{1,0:T(8,128)(2,1)} %param.5), channel_id=1, source_target_pairs={{0,3},{1,0},{2,1},{3,2},{4,7},{5,4},{6,5},{7,6},{8,11},{9,8},{10,9... | collective-permute-start | bytes 4320008 | tf_op jit(solution)/shard_map/ppermute | solution.py:14
  5.8 33.2 %collective-permute-done = bf16[600,1200]{1,0:T(8,128)(2,1)S(1)} collective-permute-done((bf16[600,1200]{1,0:T(8,128)(2,1)}, bf16[600,1200]{1,0:T(8,128)(2,1)S(1)}, u32[]{:S(2)}, u32[]{:S(2)}) %collective-permute-start) | collective-permute-done | bytes 1440032 | tf_op jit(solution)/shard_map/ppermute | solution.py:14
  38.9 4.2 %collective-permute-start.1 = (bf16[600,1200]{1,0:T(8,128)(2,1)S(1)}, bf16[600,1200]{1,0:T(8,128)(2,1)}, u32[]{:S(2)}, u32[]{:S(2)}) collective-permute-start(bf16[600,1200]{1,0:T(8,128)(2,1)S(1)} %collective-permute-done), channel_id=1, source_target_pairs={{0,3},{1,0},{2,1},{3,2},{4,7},{5,4},{6,5},{7,6},{8,11},{9,8},{10,9... | collective-permute-start | bytes 4320008 | tf_op jit(solution)/shard_map/ppermute | solution.py:14
  43.1 0.0 collective-permute-start.3
  43.1 32.0 %collective-permute-done.1 = bf16[600,1200]{1,0:T(8,128)(2,1)} collective-permute-done((bf16[600,1200]{1,0:T(8,128)(2,1)S(1)}, bf16[600,1200]{1,0:T(8,128)(2,1)}, u32[]{:S(2)}, u32[]{:S(2)}) %collective-permute-start.1) | collective-permute-done | bytes 1440032 | tf_op jit(solution)/shard_map/ppermute | solution.py:14
  75.1 4.4 %collective-permute-start.2 = (bf16[600,1200]{1,0:T(8,128)(2,1)}, bf16[600,1200]{1,0:T(8,128)(2,1)}, u32[]{:S(2)}, u32[]{:S(2)}) collective-permute-start(bf16[600,1200]{1,0:T(8,128)(2,1)} %collective-permute-done.1), channel_id=1, source_target_pairs={{0,3},{1,0},{2,1},{3,2},{4,7},{5,4},{6,5},{7,6},{8,11},{9,8},{10,9... | collective-permute-start | bytes 4320008 | tf_op jit(solution)/shard_map/ppermute | solution.py:14
  79.5 0.0 collective-permute-done.3
  79.5 0.0 copy-done.10
  79.5 0.1 collective-permute-start.5
  79.6 3.0 %convert.2 = f32[1200,400]{0,1:T(8,128)} convert(bf16[1200,400]{0,1:T(8,128)(2,1)} %param.6) | non-fusion elementwise | flops 480000 | bytes 2880000
  82.6 3.7 %fusion.18 = f32[2,400,1200]{2,1,0:T(8,128)S(1)} fusion(bf16[600,1200]{1,0:T(8,128)(2,1)} %param.5, bf16[2,400,2400]{2,1,0:T(8,128)(2,1)} %param.4, s32[]{:T(128)S(6)} %select_n.58), kind=kOutput, calls=%fused_computation.34 | convolution fusion | flops 1152000000 | bytes 6400004 | tf_op jit(solution)/shard_map/mp,wim->pwi/dot_general | solution.py:31
  86.3 0.0 copy-done.5
  86.3 0.0 copy-done.9
  86.3 0.0 copy-done.11
  86.3 1.8 fusion.16
  88.2 0.0 copy-start.3
  88.2 6.2 %collective-permute-done.5 = bf16[1200,400]{0,1:T(8,128)(2,1)S(1)} collective-permute-done((bf16[1200,400]{0,1:T(8,128)(2,1)S(1)}, bf16[1200,400]{0,1:T(8,128)(2,1)S(1)}, u32[]{:S(2)}, u32[]{:S(2)}) %collective-permute-start.5) | collective-permute-done | bytes 960032 | tf_op jit(solution)/shard_map/ppermute | solution.py:22
  94.4 0.0 collective-permute-start.7
  94.4 3.6 %fusion.14 = f32[2,400,1200]{2,1,0:T(8,128)S(1)} fusion(bf16[600,1200]{1,0:T(8,128)(2,1)} %collective-permute-done.1, bf16[2,400,2400]{2,1,0:T(8,128)(2,1)S(1)} %copy-done.9, s32[]{:T(128)S(6)} %select_n.62), kind=kOutput, calls=%fused_computation.30 | convolution fusion | flops 1152000000 | bytes 6304004 | tf_op jit(solution)/shard_map/mp,wim->pwi/dot_general | solution.py:31
  98.0 12.9 %collective-permute-done.2 = bf16[600,1200]{1,0:T(8,128)(2,1)} collective-permute-done((bf16[600,1200]{1,0:T(8,128)(2,1)}, bf16[600,1200]{1,0:T(8,128)(2,1)}, u32[]{:S(2)}, u32[]{:S(2)}) %collective-permute-start.2) | collective-permute-done | bytes 1440032 | tf_op jit(solution)/shard_map/ppermute | solution.py:14
  111.0 0.0 copy-done.3
  111.0 3.6 %multiply_reduce_fusion = (f32[1200,2]{0,1:T(2,128)S(1)}, bf16[2,400,1200]{2,1,0:T(8,128)(2,1)S(1)}) fusion(f32[1200,400]{0,1:T(8,128)S(1)} %copy-done.3, bf16[600,1200]{1,0:T(8,128)(2,1)} %collective-permute-done.2, bf16[2,400,2400]{2,1,0:T(8,128)(2,1)S(1)} %copy-done.9, s32[]{:T(128)S(6)} %select_n.64, f32[2,400,1200]{2,1,0:T(8,128)S(1)} %fusion.14, ...), kind=kOutput, calls=%fused_computation.18 | convolution fusion | flops 1158717568 | bytes 18729604 | tf_op jit(solution)/shard_map/mp,wim->pwi/dot_general | solution.py:31
  114.6 0.0 copy-done.7
  114.6 0.0 copy-start
  114.6 0.1 collective-permute-start.4
  114.7 18.1 %dynamic-slice_convert_fusion.3 = (f32[1200,1200]{1,0:T(8,128)}, f32[1200,1200]{1,0:T(8,128)}, f32[1200,1200]{1,0:T(8,128)}, f32[1200,1200]{1,0:T(8,128)}, f32[1200,1200]{1,0:T(8,128)}) fusion(bf16[1200,9600]{1,0:T(8,128)(2,1)} %param.7, s32[]{:T(128)S(6)} %select_n.67, s32[]{:T(128)S(6)} %select_n.69, s32[]{:T(128)S(6)} %select_n.65, s32[]{:T(128)S(6)} %select_n.73, ...), kind=kLoop, calls=%fused_computation.23 | loop fusion | flops 7200000 | bytes 43200020 | tf_op jit(solution)/shard_map/convert_element_type | solution.py:46
  132.8 7.9 %copy.21 = f32[1200,1200]{0,1:T(8,128)} copy(f32[1200,1200]{1,0:T(8,128)} %get-tuple-element.7) | data formatting | bytes 11520000 | tf_op jit(solution)/shard_map/convert_element_type | solution.py:46
  140.7 0.0 collective-permute-done.7
  140.7 0.9 collective-permute-start.9
  141.6 16.7 %all-gather = bf16[8,1200,2]{1,2,0:T(2,128)(2,1)S(1)} all-gather(bf16[1,1200,2]{1,2,0:T(2,128)(2,1)S(1)} %fusion.35), channel_id=1, replica_groups=mesh['pts'=8,'wlk'=4] {'pts'}, dimensions={0}, use_global_device_ids=true | all-gather | bytes 43200 | tf_op jit(solution)/shard_map/all_gather | solution.py:51
  158.3 0.2 reshape.12
  158.4 0.0 copy-start.4
  158.5 11.5 %fusion.34 = (f32[2]{0:T(128)S(1)}, f32[2,1200]{1,0:T(2,128)}) fusion(f32[1200,2]{0,1:T(2,128)S(1)} %get-tuple-element.10, bf16[9600,2]{0,1:T(2,128)(2,1)S(1)} %reshape.12, bf16[1200,9600]{1,0:T(8,128)(2,1)} %param.7), kind=kOutput, calls=%fused_computation.52 | convolution fusion | flops 46084800 | bytes 23097608 | tf_op jit(solution)/shard_map/wq,aq->wa/dot_general | solution.py:52
  170.0 0.0 collective-permute-done.4
  170.0 0.2 collective-permute-start.6
  170.2 0.0 copy-done.4
  170.2 6.3 %fusion.28 = f32[1200,2,1200]{2,0,1:T(8,128)} fusion(bf16[1200,400]{0,1:T(8,128)(2,1)S(1)} %copy-done.4, bf16[2,400,1200]{2,1,0:T(8,128)(2,1)S(1)} %get-tuple-element.11), kind=kOutput, calls=%fused_computation.44 | convolution fusion | flops 2304000000 | bytes 14400000 | tf_op jit(solution)/shard_map/awi,bi->wab/dot_general | solution.py:42
  176.5 13.4 %copy.22 = f32[1200,2,1200]{0,2,1:T(8,128)} copy(f32[1200,2,1200]{2,0,1:T(8,128)} %fusion.28) | data formatting | bytes 23040000 | tf_op jit(solution)/shard_map/awi,bi->wab/dot_general | solution.py:42
  189.9 10.9 %fusion.8 = f32[2]{0:T(128)S(1)} fusion(f32[1200,2,1200]{2,0,1:T(8,128)} %fusion.28, f32[1200,2,1200]{0,2,1:T(8,128)} %copy.22, f32[1200,1200]{0,1:T(8,128)} %copy.21), kind=kLoop, calls=%fused_computation.17 | loop fusion | flops 8639998 | bytes 28800008 | tf_op jit(solution)/shard_map/reduce_sum | solution.py:49
  200.8 0.0 collective-permute-done.6
  200.8 1.5 collective-permute-start.8
  202.3 8.0 %convolution_bitcast_fusion.3 = f32[2,1200,1200]{2,1,0:T(8,128)} fusion(bf16[1200,2,400]{0,2,1:T(8,128)(2,1)} %collective-permute-done.4, bf16[1200,400]{0,1:T(8,128)(2,1)S(1)} %copy-done.4), kind=kOutput, calls=%fused_computation.15 | convolution fusion | flops 2304000000 | bytes 14400000 | tf_op jit(solution)/shard_map/ai,bwi->wab/dot_general | solution.py:43
  210.3 0.0 copy-done
  210.3 0.0 slice-done.6
  210.3 0.0 slice-done.7
  210.3 0.0 copy-done.6
  210.3 0.0 slice-start.4
  210.4 8.6 %fusion.12 = f32[2]{0:T(128)S(1)} fusion(f32[2,1200,1200]{2,1,0:T(8,128)} %convolution_bitcast_fusion.3, f32[1200,1200]{1,0:T(8,128)S(1)} %bitcast.115, bf16[1200,400]{0,1:T(8,128)(2,1)S(1)} %copy-done.6, bf16[2,400,1200]{2,1,0:T(8,128)(2,1)S(1)} %get-tuple-element.11), kind=kOutput, calls=%fused_computation.28 | convolution fusion | flops 2312640000 | bytes 20160008 | tf_op jit(solution)/shard_map/awi,bi->wab/dot_general | solution.py:42
  218.9 8.2 %convolution_bitcast_fusion.2 = f32[2,1200,1200]{2,1,0:T(8,128)} fusion(bf16[1200,2,400]{0,2,1:T(8,128)(2,1)} %collective-permute-done.6, bf16[1200,400]{0,1:T(8,128)(2,1)S(1)} %copy-done.4), kind=kOutput, calls=%fused_computation.14 | convolution fusion | flops 2304000000 | bytes 14400000 | tf_op jit(solution)/shard_map/ai,bwi->wab/dot_general | solution.py:43
  227.1 0.0 collective-permute-done.8
  227.1 0.3 collective-permute-start.10
  227.5 0.0 slice-done.4
  227.5 0.0 slice-done.5
  227.5 0.0 slice-start.2
  227.5 8.6 %fusion.11 = f32[2]{0:T(128)S(1)} fusion(f32[2,1200,1200]{2,1,0:T(8,128)} %convolution_bitcast_fusion.2, f32[1200,1200]{1,0:T(8,128)S(1)} %bitcast.113, bf16[1200,400]{0,1:T(8,128)(2,1)S(1)} %copy-done.8, bf16[2,400,1200]{2,1,0:T(8,128)(2,1)S(1)} %copy-done.1), kind=kOutput, calls=%fused_computation.27 | convolution fusion | flops 2312640000 | bytes 20160008 | tf_op jit(solution)/shard_map/awi,bi->wab/dot_general | solution.py:42
  236.1 8.2 %convolution_bitcast_fusion.1 = f32[2,1200,1200]{2,1,0:T(8,128)} fusion(bf16[1200,2,400]{0,2,1:T(8,128)(2,1)} %collective-permute-done.8, bf16[1200,400]{0,1:T(8,128)(2,1)S(1)} %copy-done.4), kind=kOutput, calls=%fused_computation.13 | convolution fusion | flops 2304000000 | bytes 14400000 | tf_op jit(solution)/shard_map/ai,bwi->wab/dot_general | solution.py:43
  244.3 0.0 slice-done.3
  244.3 0.0 slice-start
  244.3 8.9 %fusion.10 = f32[2]{0:T(128)S(1)} fusion(f32[2,1200,1200]{2,1,0:T(8,128)} %convolution_bitcast_fusion.1, f32[1200,1200]{1,0:T(8,128)S(1)} %bitcast.111, bf16[1200,400]{0,1:T(8,128)(2,1)} %collective-permute-done.7, bf16[2,400,1200]{2,1,0:T(8,128)(2,1)S(1)} %copy-done.2), kind=kOutput, calls=%fused_computation.26 | convolution fusion | flops 2312640000 | bytes 20160008 | tf_op jit(solution)/shard_map/awi,bi->wab/dot_general | solution.py:42
  253.2 0.1 collective-permute-done.10
  253.3 8.1 %convolution_bitcast_fusion = f32[2,1200,1200]{2,1,0:T(8,128)} fusion(bf16[1200,2,400]{0,2,1:T(8,128)(2,1)} %collective-permute-done.10, bf16[1200,400]{0,1:T(8,128)(2,1)S(1)} %copy-done.4), kind=kOutput, calls=%fused_computation.12 | convolution fusion | flops 2304000000 | bytes 14400000 | tf_op jit(solution)/shard_map/ai,bwi->wab/dot_general | solution.py:43
  261.4 0.0 collective-permute-done.9
  261.5 8.7 %fusion.9 = f32[2]{0:T(128)S(1)} fusion(f32[2,1200,1200]{2,1,0:T(8,128)} %convolution_bitcast_fusion, f32[1200,1200]{1,0:T(8,128)S(1)} %bitcast.109, bf16[1200,400]{0,1:T(8,128)(2,1)} %collective-permute-done.9, bf16[2,400,1200]{2,1,0:T(8,128)(2,1)S(1)} %copy-done.2), kind=kOutput, calls=%fused_computation.25 | convolution fusion | flops 2312640000 | bytes 20160008 | tf_op jit(solution)/shard_map/awi,bi->wab/dot_general | solution.py:42
  270.2 14.6 %all-reduce = (f32[2]{0:T(128)}, f32[2]{0:T(128)}) all-reduce(f32[2]{0:T(128)S(1)} %broadcast_multiply_fusion, f32[2]{0:T(128)S(1)} %add_multiply_fusion), channel_id=1, replica_groups=mesh['pts'=8,'wlk'=4] {'pts'}, use_global_device_ids=true, to_apply=%region_1.2 | all-reduce | flops 4 | bytes 32 | tf_op jit(solution)/shard_map/psum | solution.py:63
  (28 shorter events, 0.1 us)
Async XLA Ops:
  0.6 38.3 %collective-permute-start = (bf16[600,1200]{1,0:T(8,128)(2,1)}, bf16[600,1200]{1,0:T(8,128)(2,1)S(1)}, u32[]{:S(2)}, u32[]{:S(2)}) collective-permute-start(bf16[600,1200]{1,0:T(8,128)(2,1)} %param.5), channel_id=1, source_target_pairs={{0,3},{1,0},{2,1},{3,2},{4,7},{5,4},{6,5},{7,6},{8,11},{9,8},{10,9... | collective-permute-start | bytes 4320008 | tf_op jit(solution)/shard_map/ppermute | solution.py:14
  38.9 40.6 %copy-start.10 = (bf16[600,1200]{1,0:T(8,128)(2,1)}, bf16[600,1200]{1,0:T(8,128)(2,1)S(1)}, u32[]{:S(2)}) copy-start(bf16[600,1200]{1,0:T(8,128)(2,1)S(1)} %collective-permute-done) | copy-start | bytes 4320004
  38.9 36.2 %collective-permute-start.1 = (bf16[600,1200]{1,0:T(8,128)(2,1)S(1)}, bf16[600,1200]{1,0:T(8,128)(2,1)}, u32[]{:S(2)}, u32[]{:S(2)}) collective-permute-start(bf16[600,1200]{1,0:T(8,128)(2,1)S(1)} %collective-permute-done), channel_id=1, source_target_pairs={{0,3},{1,0},{2,1},{3,2},{4,7},{5,4},{6,5},{7,6},{8,11},{9,8},{10,9... | collective-permute-start | bytes 4320008 | tf_op jit(solution)/shard_map/ppermute | solution.py:14
  43.1 36.4 %collective-permute-start.3 = (bf16[1200,400]{0,1:T(8,128)(2,1)}, bf16[1200,400]{0,1:T(8,128)(2,1)S(1)}, u32[]{:S(2)}, u32[]{:S(2)}) collective-permute-start(bf16[1200,400]{0,1:T(8,128)(2,1)} %param.6), channel_id=1, source_target_pairs={{28,0},{0,4},{4,8},{8,12},{12,16},{16,20},{20,24},{24,28},{29,1},{... | collective-permute-start | bytes 2880008 | tf_op jit(solution)/shard_map/ppermute | solution.py:22
  75.1 35.9 %collective-permute-start.2 = (bf16[600,1200]{1,0:T(8,128)(2,1)}, bf16[600,1200]{1,0:T(8,128)(2,1)}, u32[]{:S(2)}, u32[]{:S(2)}) collective-permute-start(bf16[600,1200]{1,0:T(8,128)(2,1)} %collective-permute-done.1), channel_id=1, source_target_pairs={{0,3},{1,0},{2,1},{3,2},{4,7},{5,4},{6,5},{7,6},{8,11},{9,8},{10,9... | collective-permute-start | bytes 4320008 | tf_op jit(solution)/shard_map/ppermute | solution.py:14
  79.5 6.8 %copy-start.5 = (bf16[1200,400]{0,1:T(8,128)(2,1)}, bf16[1200,400]{0,1:T(8,128)(2,1)S(1)}, u32[]{:S(2)}) copy-start(bf16[1200,400]{0,1:T(8,128)(2,1)S(1)} %collective-permute-done.3) | copy-start | bytes 2880004
  79.5 14.9 %collective-permute-start.5 = (bf16[1200,400]{0,1:T(8,128)(2,1)S(1)}, bf16[1200,400]{0,1:T(8,128)(2,1)S(1)}, u32[]{:S(2)}, u32[]{:S(2)}) collective-permute-start(bf16[1200,400]{0,1:T(8,128)(2,1)S(1)} %collective-permute-done.3), channel_id=1, source_target_pairs={{28,0},{0,4},{4,8},{8,12},{12,16},{16,20},{20,24},{24,28},{29,1},{... | collective-permute-start | bytes 2880008 | tf_op jit(solution)/shard_map/ppermute | solution.py:22
  82.6 3.8 %copy-start.9 = (bf16[2,400,2400]{2,1,0:T(8,128)(2,1)S(1)}, bf16[2,400,2400]{2,1,0:T(8,128)(2,1)}, u32[]{:S(2)}) copy-start(bf16[2,400,2400]{2,1,0:T(8,128)(2,1)} %param.4) | copy-start | bytes 11520004
  82.6 3.8 %copy-start.11 = (bf16[600,1200]{1,0:T(8,128)(2,1)S(1)}, bf16[600,1200]{1,0:T(8,128)(2,1)}, u32[]{:S(2)}) copy-start(bf16[600,1200]{1,0:T(8,128)(2,1)} %copy-done.10) | copy-start | bytes 4320004
  88.2 22.8 %copy-start.3 = (f32[1200,400]{0,1:T(8,128)S(1)}, f32[1200,400]{0,1:T(8,128)}, u32[]{:S(2)}) copy-start(f32[1200,400]{0,1:T(8,128)} %convert.2) | copy-start | bytes 5760004
  94.4 20.2 %copy-start.7 = (bf16[1200,400]{0,1:T(8,128)(2,1)}, bf16[1200,400]{0,1:T(8,128)(2,1)S(1)}, u32[]{:S(2)}) copy-start(bf16[1200,400]{0,1:T(8,128)(2,1)S(1)} %collective-permute-done.5) | copy-start | bytes 2880004
  94.4 46.2 %collective-permute-start.7 = (bf16[1200,400]{0,1:T(8,128)(2,1)S(1)}, bf16[1200,400]{0,1:T(8,128)(2,1)}, u32[]{:S(2)}, u32[]{:S(2)}) collective-permute-start(bf16[1200,400]{0,1:T(8,128)(2,1)S(1)} %collective-permute-done.5), channel_id=1, source_target_pairs={{28,0},{0,4},{4,8},{8,12},{12,16},{16,20},{20,24},{24,28},{29,1},{... | collective-permute-start | bytes 2880008 | tf_op jit(solution)/shard_map/ppermute | solution.py:22
  114.6 95.7 %copy-start = (bf16[2,400,1200]{2,1,0:T(8,128)(2,1)}, bf16[2,400,1200]{2,1,0:T(8,128)(2,1)S(1)}, u32[]{:S(2)}) copy-start(bf16[2,400,1200]{2,1,0:T(8,128)(2,1)S(1)} %get-tuple-element.11) | copy-start | bytes 5760004
  114.6 55.3 %collective-permute-start.4 = (bf16[1200,2,400]{0,2,1:T(8,128)(2,1)S(1)}, bf16[1200,2,400]{0,2,1:T(8,128)(2,1)}, u32[]{:S(2)}, u32[]{:S(2)}) collective-permute-start(bf16[1200,2,400]{0,2,1:T(8,128)(2,1)S(1)} %bitcast.116), channel_id=1, source_target_pairs={{28,0},{0,4},{4,8},{8,12},{12,16},{16,20},{20,24},{24,28},{29,1},{... | collective-permute-start | bytes 5760008 | tf_op jit(solution)/shard_map/ppermute | solution.py:22
  140.7 120.8 %collective-permute-start.9 = (bf16[1200,400]{0,1:T(8,128)(2,1)}, bf16[1200,400]{0,1:T(8,128)(2,1)}, u32[]{:S(2)}, u32[]{:S(2)}) collective-permute-start(bf16[1200,400]{0,1:T(8,128)(2,1)} %collective-permute-done.7), channel_id=1, source_target_pairs={{28,0},{0,4},{4,8},{8,12},{12,16},{16,20},{20,24},{24,28},{29,1},{... | collective-permute-start | bytes 2880008 | tf_op jit(solution)/shard_map/ppermute | solution.py:22
  158.4 11.7 %copy-start.4 = (bf16[1200,400]{0,1:T(8,128)(2,1)S(1)}, bf16[1200,400]{0,1:T(8,128)(2,1)}, u32[]{:S(2)}) copy-start(bf16[1200,400]{0,1:T(8,128)(2,1)} %param.6) | copy-start | bytes 2880004
  170.0 30.9 %collective-permute-start.6 = (bf16[1200,2,400]{0,2,1:T(8,128)(2,1)}, bf16[1200,2,400]{0,2,1:T(8,128)(2,1)}, u32[]{:S(2)}, u32[]{:S(2)}) collective-permute-start(bf16[1200,2,400]{0,2,1:T(8,128)(2,1)} %collective-permute-done.4), channel_id=1, source_target_pairs={{28,0},{0,4},{4,8},{8,12},{12,16},{16,20},{20,24},{24,28},{29,1},{... | collective-permute-start | bytes 5760008 | tf_op jit(solution)/shard_map/ppermute | solution.py:22
  189.9 20.4 %slice-start.6 = ((s8[6144000]{0:T(1024)(128)(4,1)}), s8[4194304]{0:T(1024)(128)(4,1)S(1)}, s32[]{:S(2)}) async-start(s8[6144000]{0:T(1024)(128)(4,1)} %bitcast.114), calls=%async_computation.6 | async-start | bytes 8388608
  200.8 9.5 %slice-start.7 = ((s8[6144000]{0:T(1024)(128)(4,1)}), s8[1949696]{0:T(1024)(128)(4,1)S(1)}, s32[]{:S(2)}) async-start(s8[6144000]{0:T(1024)(128)(4,1)} %bitcast.114), calls=%async_computation.7 | async-start | bytes 3899392
  200.8 9.5 %copy-start.6 = (bf16[1200,400]{0,1:T(8,128)(2,1)S(1)}, bf16[1200,400]{0,1:T(8,128)(2,1)}, u32[]{:S(2)}) copy-start(bf16[1200,400]{0,1:T(8,128)(2,1)} %copy-done.5) | copy-start | bytes 2880004
  200.8 26.3 %collective-permute-start.8 = (bf16[1200,2,400]{0,2,1:T(8,128)(2,1)}, bf16[1200,2,400]{0,2,1:T(8,128)(2,1)}, u32[]{:S(2)}, u32[]{:S(2)}) collective-permute-start(bf16[1200,2,400]{0,2,1:T(8,128)(2,1)} %collective-permute-done.6), channel_id=1, source_target_pairs={{28,0},{0,4},{4,8},{8,12},{12,16},{16,20},{20,24},{24,28},{29,1},{... | collective-permute-start | bytes 5760008 | tf_op jit(solution)/shard_map/ppermute | solution.py:22
  210.3 17.1 %slice-start.4 = ((s8[6144000]{0:T(1024)(128)(4,1)}), s8[4194304]{0:T(1024)(128)(4,1)S(1)}, s32[]{:S(2)}) async-start(s8[6144000]{0:T(1024)(128)(4,1)} %bitcast.112), calls=%async_computation.4 | async-start | bytes 8388608
  218.9 8.5 %slice-start.5 = ((s8[6144000]{0:T(1024)(128)(4,1)}), s8[1949696]{0:T(1024)(128)(4,1)S(1)}, s32[]{:S(2)}) async-start(s8[6144000]{0:T(1024)(128)(4,1)} %bitcast.112), calls=%async_computation.5 | async-start | bytes 3899392
  218.9 8.5 %copy-start.1 = (bf16[2,400,1200]{2,1,0:T(8,128)(2,1)S(1)}, bf16[2,400,1200]{2,1,0:T(8,128)(2,1)}, u32[]{:S(2)}) copy-start(bf16[2,400,1200]{2,1,0:T(8,128)(2,1)} %copy-done) | copy-start | bytes 5760004
  218.9 8.5 %copy-start.8 = (bf16[1200,400]{0,1:T(8,128)(2,1)S(1)}, bf16[1200,400]{0,1:T(8,128)(2,1)}, u32[]{:S(2)}) copy-start(bf16[1200,400]{0,1:T(8,128)(2,1)} %copy-done.7) | copy-start | bytes 2880004
  227.1 26.1 %collective-permute-start.10 = (bf16[1200,2,400]{0,2,1:T(8,128)(2,1)}, bf16[1200,2,400]{0,2,1:T(8,128)(2,1)}, u32[]{:S(2)}, u32[]{:S(2)}) collective-permute-start(bf16[1200,2,400]{0,2,1:T(8,128)(2,1)} %collective-permute-done.8), channel_id=1, source_target_pairs={{28,0},{0,4},{4,8},{8,12},{12,16},{16,20},{20,24},{24,28},{29,1},{... | collective-permute-start | bytes 5760008 | tf_op jit(solution)/shard_map/ppermute | solution.py:22
  227.5 16.8 %slice-start.2 = ((s8[6144000]{0:T(1024)(128)(4,1)}), s8[4194304]{0:T(1024)(128)(4,1)S(1)}, s32[]{:S(2)}) async-start(s8[6144000]{0:T(1024)(128)(4,1)} %bitcast.110), calls=%async_computation.2 | async-start | bytes 8388608
  236.1 8.2 %slice-start.3 = ((s8[6144000]{0:T(1024)(128)(4,1)}), s8[1949696]{0:T(1024)(128)(4,1)S(1)}, s32[]{:S(2)}) async-start(s8[6144000]{0:T(1024)(128)(4,1)} %bitcast.110), calls=%async_computation.3 | async-start | bytes 3899392
  236.1 8.2 %copy-start.2 = (bf16[2,400,1200]{2,1,0:T(8,128)(2,1)S(1)}, bf16[2,400,1200]{2,1,0:T(8,128)(2,1)}, u32[]{:S(2)}) copy-start(bf16[2,400,1200]{2,1,0:T(8,128)(2,1)} %copy-done) | copy-start | bytes 5760004
  244.3 17.1 %slice-start = ((s8[6144000]{0:T(1024)(128)(4,1)}), s8[4194304]{0:T(1024)(128)(4,1)S(1)}, s32[]{:S(2)}) async-start(s8[6144000]{0:T(1024)(128)(4,1)} %bitcast.108), calls=%async_computation | async-start | bytes 8388608
  253.2 8.2 %slice-start.1 = ((s8[6144000]{0:T(1024)(128)(4,1)}), s8[1949696]{0:T(1024)(128)(4,1)S(1)}, s32[]{:S(2)}) async-start(s8[6144000]{0:T(1024)(128)(4,1)} %bitcast.108), calls=%async_computation.1 | async-start | bytes 3899392
